TPU v7x, 32 devices: a whole 2x2x4 slice. The times are simulated.
32 devices in a mesh: dp: 4 (over y, x), seq: 8 (over z, core).
Axes of the slice: x: 2, y: 2, z: 4, core: 2. Of those that a mesh axis runs over, the one named last changes fastest.
Arguments:
- stream: bfloat16 [4, 256, 1536], P('dp', 'seq'), may hold values from -6 to 6
- queries: bfloat16 [4, 256, 1536], P('dp', 'seq'), may hold values from -30 to 30
- new_keys: bfloat16 [4, 256, 1536], P('dp', 'seq'), may hold values from -6.5 to 6.5
- new_values: bfloat16 [4, 256, 1536], P('dp', 'seq'), may hold values from -6 to 6
- cache_keys: bfloat16 [4, 768, 1536], P('dp', 'seq'), may hold values from -6.375 to 6.375
- cache_values: bfloat16 [4, 768, 1536], P('dp', 'seq'), may hold values from -6 to 6
- cache_frames: int32 [4, 768], P('dp', 'seq'), may hold values from 0 to 20, as said below
- group_index: int32 [4], P('dp'), may hold values from 4 to 7, as said below
- timestep: int32 [4], P('dp'), may hold values from 0 to 3
- gate_table: float32 [4, 1536], replicated, may hold values from 0.1 to 1.9
- attn_out_weight: bfloat16 [1536, 1536], replicated, may hold values from -0.15625 to 0.15625
- critic_in: bfloat16 [32768, 1536], P(('dp', 'seq')), may hold values from -6 to 6
- critic_cot: bfloat16 [32768, 1536], P(('dp', 'seq')), may hold values from -6 to 6
- critic_weight: bfloat16 [1536, 1536], P(('dp', 'seq')), may hold values from -0.15625 to 0.15625
Outputs:
- stream_out: bfloat16 [4, 256, 1536], P('dp', 'seq')
- critic_grad_in: bfloat16 [32768, 1536], P(('dp', 'seq'))
- critic_grad_weight: float32 [1536, 1536], P(('dp', 'seq'))
Inputs may be any that keep to these rules, and one draw needn't show every extreme that they name: `group_index`: index of the frame group; both ends are reached in every draw. `cache_frames`: sample b's cache holds the 12 frames 3 * group_index[b] - 12 to 3 * group_index[b] - 1, each in one contiguous run of slots, runs of equal length up to one slot, in a rotated order.
All inputs are finite; a program needn't handle non-finite values.
Results may differ from a plain program's by a relative error of at most 0.0045.
Values may be sent and summed in bfloat16 or wider, within the bound.
A program may use at most 128 MiB of HBM per device.

v0:
```python
import jax
import jax.numpy as jnp
from jax import lax
from jax.sharding import PartitionSpec as P

HEADS = 12
HEAD = 128
FRAMES_GROUP = 3
WINDOW_FRAMES = 9


def critic_pass(critic_in, critic_cot, critic_weight):
    grad_in = lax.dot_general(
        critic_cot,
        lax.all_gather(critic_weight, ("dp", "seq"), axis=0, tiled=True),
        (((1,), (1,)), ((), ())),
        preferred_element_type=jnp.float32,
    ).astype(jnp.bfloat16)
    factor = float(critic_in.shape[0] * lax.axis_size(("dp", "seq"))) ** (-0.5)
    whole_term = (
        lax.dot_general(
            critic_in, critic_cot, (((0,), (0,)), ((), ())), preferred_element_type=jnp.float32
        )
        * factor
    )
    grad_weight = lax.psum_scatter(whole_term, ("dp", "seq"), scatter_dimension=0, tiled=True)
    return (grad_in, grad_weight)


def local(
    stream,
    queries,
    new_keys,
    new_values,
    cache_keys,
    cache_values,
    cache_frames,
    group_index,
    timestep,
    gate_table,
    attn_out_weight,
    critic_in,
    critic_cot,
    critic_weight,
):
    query_local = queries[0]
    own_rows = query_local.shape[0]
    width = query_local.shape[1]
    scale = HEAD ** (-0.5)
    first_frame = FRAMES_GROUP * group_index[0]
    frames = cache_frames[0]
    live_cache = (frames < first_frame) & (frames >= first_frame - WINDOW_FRAMES)
    live_local = jnp.concatenate([live_cache, jnp.ones((own_rows,), dtype=bool)])
    keys_local = jnp.concatenate([cache_keys[0], new_keys[0]], axis=0)
    values_local = jnp.concatenate([cache_values[0], new_values[0]], axis=0)
    all_queries = lax.all_gather(queries, "seq", axis=1, tiled=True)[0]
    total_rows = all_queries.shape[0]
    query_heads = all_queries.reshape(total_rows, HEADS, HEAD)
    key_heads = keys_local.reshape(-1, HEADS, HEAD)
    value_heads = values_local.reshape(-1, HEADS, HEAD)
    scores = (
        jnp.einsum("qhd,khd->hqk", query_heads, key_heads, preferred_element_type=jnp.float32)
        * scale
    )
    scores = jnp.where(live_local[None, None, :], scores, -1e30)
    local_top = jnp.max(scores, axis=2)
    global_top = lax.pmax(local_top, "seq")
    weights = jnp.where(live_local[None, None, :], jnp.exp(scores - global_top[:, :, None]), 0.0)
    totals = jnp.sum(weights, axis=2)
    summed = jnp.einsum(
        "hqk,khd->qhd",
        weights.astype(jnp.bfloat16),
        value_heads,
        preferred_element_type=jnp.float32,
    )
    own_sums, own_totals = (
        lax.psum_scatter(summed.reshape(total_rows, width), "seq", scatter_dimension=0, tiled=True),
        lax.psum_scatter(totals.T, "seq", scatter_dimension=0, tiled=True),
    )
    mixed = (
        (own_sums.reshape(own_rows, HEADS, HEAD) / own_totals[:, :, None])
        .reshape(own_rows, width)
        .astype(jnp.bfloat16)
    )
    projected = jnp.dot(mixed, attn_out_weight, preferred_element_type=jnp.float32)
    onehot = (
        timestep[:, None] == jnp.arange(gate_table.shape[0], dtype=jnp.int32)[None, :]
    ).astype(jnp.float32)
    gate = jnp.dot(onehot, gate_table, precision=lax.Precision.HIGHEST)
    stream_out = (stream[0].astype(jnp.float32) + gate * projected).astype(jnp.bfloat16)[None]
    grad_in, grad_weight = critic_pass(critic_in, critic_cot, critic_weight)
    return (stream_out, grad_in, grad_weight)


def solution(mesh):
    return jax.shard_map(
        local,
        mesh=mesh,
        in_specs=(
            P("dp", "seq", None),
            P("dp", "seq", None),
            P("dp", "seq", None),
            P("dp", "seq", None),
            P("dp", "seq", None),
            P("dp", "seq", None),
            P("dp", "seq"),
            P("dp"),
            P("dp"),
            P(),
            P(),
            P(("dp", "seq"), None),
            P(("dp", "seq"), None),
            P(("dp", "seq"), None),
        ),
        out_specs=(P("dp", "seq", None), P(("dp", "seq"), None), P(("dp", "seq"), None)),
        check_vma=False,
    )
```

profile of v0, /device:TPU:9, one launch (start us, length us, event | category | flops | bytes accessed | tf_op | source)
XLA Modules:
  0.0 283.2 jit_solution(722944239257514298)
XLA Ops:
  8.0 0.0 copy-start
  8.0 0.0 copy-start.4
  8.0 0.0 reduce-scatter.12.cloned.1.call-start
  8.9 17.4 %all_gather.6 = bf16[1,256,1536]{2,1,0:T(8,128)(2,1)} all-gather(bf16[1,32,1536]{2,1,0:T(8,128)(2,1)} %param.15), channel_id=1, replica_groups=mesh['dp'=4,'seq'=8] {'seq'}, dimensions={1}, use_global_device_ids=true | all-gather | bytes 884736 | tf_op jit(solution)/shard_map/all_gather | solution.py:56
  26.2 2.3 copy.31
  28.5 1.2 concatenate.23
  29.7 0.8 copy.29
  30.5 1.0 concatenate.24
  31.5 0.0 copy-done.4
  31.6 0.0 copy-start.3
  31.6 2.7 bitcast_reduce_fusion
  34.3 21.6 %pmax.7 = f32[12,256]{1,0:T(8,128)S(1)} all-reduce(f32[12,256]{1,0:T(8,128)S(1)} %get-tuple-element.3), channel_id=1, replica_groups=mesh['dp'=4,'seq'=8] {'seq'}, use_global_device_ids=true, to_apply=%region_1.2 | all-reduce | flops 3072 | bytes 24576 | tf_op jit(solution)/shard_map/pmax | solution.py:67
  56.0 1.7 fusion.5
  57.7 0.8 copy.38
  58.4 0.0 reduce-scatter.12.cloned.1.call-update
  58.5 0.0 copy-done.3
  58.5 0.0 reduce-scatter.10.cloned.1.call-start
  58.5 1.2 copy.27
  59.7 1.8 copy.28
  61.5 3.2 %fusion.7 = f32[12,128,256]{2,1,0:T(8,128)} fusion(f32[12,128,256]{2,1,0:T(8,128)} %get-tuple-element.4, f32[12,256]{1,0:T(8,128)S(1)} %pmax.7, pred[128]{0:T(512)(128)(4,1)} %copy-done.3, bf16[32,12,128]{0,2,1:T(8,128)(2,1)} %bitcast.49, bf16[96,12,128]{0,2,1:T(8,128)(2,1)S(1)} %bitcast.48), kind=kOutput, calls=%fused_computation.14 | convolution fusion | flops 102629376 | bytes 3551360 | tf_op jit(solution)/shard_map/hqk,khd->qhd/dot_general | solution.py:70
  64.7 3.0 %copy.36 = f32[256,1536]{1,0:T(8,128)} copy(f32[256,1536]{0,1:T(8,128)} %bitcast.46) | data formatting | bytes 3145728
  67.7 0.0 reduce-scatter.10.cloned.1.call-update
  67.7 0.0 all-gather.2.cloned.1.call-start
  67.8 0.5 all-gather.2.cloned.1.call-update
  68.3 0.0 reduce-scatter.8.cloned.1.call-start
  68.4 0.0 copy-done
  68.4 9.6 %convolution_multiply_fusion = f32[1536,1536]{1,0:T(8,128)} fusion(bf16[1024,1536]{1,0:T(8,128)(2,1)} %param.25, bf16[1024,1536]{1,0:T(8,128)(2,1)S(1)} %copy-done), kind=kOutput, calls=%fused_computation | convolution fusion | flops 4834197504 | bytes 15728640 | tf_op jit(solution)/shard_map/dot_general | solution.py:21
  78.0 0.0 copy-start.2
  78.0 0.0 copy-start.1
  78.0 0.0 reduce-scatter.8.cloned.1.call-update
  78.7 0.0 copy-done.2
  78.7 0.2 convolution_reduce_fusion
  78.9 8.9 %reduce-scatter.12.cloned.1.call-done = f32[32,12]{1,0:T(8,128)} async-done(((f32[256,12]{1,0:T(8,128)}), f32[32,12]{1,0:T(8,128)}) %reduce-scatter.12.cloned.1.call-update) | async-done | bytes 1552
  87.8 0.8 copy.39
  88.6 41.3 %reduce-scatter.10.cloned.1.call-done = f32[32,1536]{1,0:T(8,128)} async-done(((f32[256,1536]{1,0:T(8,128)}), f32[32,1536]{1,0:T(8,128)}) %reduce-scatter.10.cloned.1.call-update) | async-done | bytes 196624
  129.9 2.1 copy.37
  132.0 1.2 fusion.9
  133.3 0.0 copy-done.1
  133.3 4.0 %fusion.2 = bf16[1,32,1536]{2,1,0:T(8,128)(2,1)} fusion(bf16[32,1536]{0,1:T(8,128)(2,1)S(1)} %fusion.9, bf16[1536,1536]{1,0:T(8,128)(2,1)} %param.24, bf16[1,32,1536]{2,1,0:T(8,128)(2,1)S(1)} %copy-done.1, f32[1536]{0:T(1024)S(1)} %convolution_reduce_fusion), kind=kOutput, calls=%fused_computation.5 | convolution fusion | flops 151191552 | bytes 5019648 | tf_op jit(solution)/shard_map/dot_general | solution.py:85
  137.3 6.1 %all-gather.2.cloned.1.call-done = bf16[1536,1536]{1,0:T(8,128)(2,1)} async-done(((bf16[48,1536]{1,0:T(8,128)(2,1)}), bf16[1536,1536]{1,0:T(8,128)(2,1)}) %all-gather.2.cloned.1.call-update) | async-done | bytes 4718608 | tf_op jit(solution)/shard_map/all_gather | solution.py:15
  143.4 8.8 %convolution_convert_fusion = bf16[1024,1536]{1,0:T(8,128)(2,1)} fusion(bf16[1024,1536]{1,0:T(8,128)(2,1)S(1)} %copy-done, bf16[1536,1536]{1,0:T(8,128)(2,1)} %all-gather.2.cloned.1.call-done), kind=kOutput, calls=%fused_computation.1 | convolution fusion | flops 4833411072 | bytes 11010048 | tf_op jit(solution)/shard_map/dot_general | solution.py:13
  152.1 123.9 %reduce-scatter.8.cloned.1.call-done = f32[48,1536]{1,0:T(8,128)} async-done(((f32[1536,1536]{1,0:T(8,128)}), f32[48,1536]{1,0:T(8,128)}) %reduce-scatter.8.cloned.1.call-update) | async-done | bytes 294928 | tf_op jit(solution)/shard_map/reduce_scatter | solution.py:26
  (3 shorter events, 0.0 us)
Async XLA Ops:
  8.0 60.4 %copy-start = (bf16[1024,1536]{1,0:T(8,128)(2,1)S(1)}, bf16[1024,1536]{1,0:T(8,128)(2,1)}, u32[]{:S(2)}) copy-start(bf16[1024,1536]{1,0:T(8,128)(2,1)} %param.26) | copy-start | bytes 9437188
  8.0 23.5 %copy-start.4 = (s32[1,96]{1,0:T(1,128)S(1)}, s32[1,96]{1,0:T(1,128)}, u32[]{:S(2)}) copy-start(s32[1,96]{1,0:T(1,128)} %param.20) | copy-start | bytes 1156
  8.0 79.8 %reduce-scatter.12.cloned.1.call-start = ((), (), s32[]{:S(2)}) async-start(), calls=%async_computation.6 | async-start | bytes 147456
  31.6 26.9 %copy-start.3 = (pred[128]{0:T(512)(128)(4,1)}, pred[128]{0:T(512)(128)(4,1)S(1)}, u32[]{:S(2)}) copy-start(pred[128]{0:T(512)(128)(4,1)S(1)} %concatenate.22) | copy-start | bytes 388
  58.5 71.5 %reduce-scatter.10.cloned.1.call-start = ((), (), s32[]{:S(2)}) async-start(), calls=%async_computation.5 | async-start | bytes 1769472
  67.7 75.6 %all-gather.2.cloned.1.call-start = ((), (), s32[]{:S(2)}) async-start(), calls=%async_computation.3 | async-start | bytes 4866048 | tf_op jit(solution)/shard_map/all_gather | solution.py:15
  68.3 207.7 %reduce-scatter.8.cloned.1.call-start = ((), (), s32[]{:S(2)}) async-start(), calls=%async_computation.4 | async-start | bytes 9732096 | tf_op jit(solution)/shard_map/reduce_scatter | solution.py:26
  78.0 0.7 copy-start.2
  78.0 55.3 %copy-start.1 = (bf16[1,32,1536]{2,1,0:T(8,128)(2,1)S(1)}, bf16[1,32,1536]{2,1,0:T(8,128)(2,1)}, u32[]{:S(2)}) copy-start(bf16[1,32,1536]{2,1,0:T(8,128)(2,1)} %param.14) | copy-start | bytes 294916
Sparse Core Ops, SparseCore 0:
  58.6 29.1 reduce-scatter.11
  90.7 39.2 reduce-scatter.9
  136.4 139.5 reduce-scatter.7
Sparse Core Ops, SparseCore 1:
  71.3 72.0 all-gather.1
where the time goes:
time: 288 us; the launch traced here: 283 us
  waiting for transfers between devices  181 us (63%)
  blocking collectives  39 us (14%)
  matrix products  28.5 us (10%)
  between operations  16.8 us (6%)
  local copies, waits for them, and re-layouts  15 us (5%)
  other arithmetic  2.93 us (1%)
    reduce_scatter x1, waiting for transfers between devices, critic_pass(): lax.psum_scatter(whole_term, ('dp', 'seq'), scatter_dimension=0, tiled=True)  124 us
    unnamed x6, waiting for transfers between devices  50.8 us
    pmax x1, blocking collectives, local(): global_top = lax.pmax(local_top, 'seq')  21.6 us
    all_gather x1, blocking collectives, local(): all_queries = lax.all_gather(queries, 'seq', axis=1, tiled=True)[0]  17.4 us
    unnamed x16, local copies, waits for them, and re-layouts  9.71 us
    dot_general x1, matrix products, critic_pass(): lax.dot_general(critic_in, critic_cot, (((0,), (0,)), ((), ())), preferre...  9.59 us
    dot_general x1, matrix products, critic_pass(): lax.dot_general(critic_cot, lax.all_gather(critic_weight, ('dp', 'seq'),...  8.76 us
    all_gather x1, waiting for transfers between devices, critic_pass(): lax.all_gather(critic_weight, ('dp', 'seq'), axis=0, tiled=True)  6.06 us
  transfers between devices with their start and end apart: 4, of which 4 were waited for; matrix products, arithmetic and copies ran while one was open for 13% of the time, Pallas kernels for 0%

commit v1 on v0

--- a/solution.py
+++ b/solution.py
@@ -1,6 +1,10 @@
+import functools
+
 import jax
 import jax.numpy as jnp
 from jax import lax
+from jax.experimental import pallas as pl
+from jax.experimental.pallas import tpu as pltpu
 from jax.sharding import PartitionSpec as P
 
 HEADS = 12
@@ -27,7 +31,7 @@
     return (grad_in, grad_weight)
 
 
-def local(
+def by_collectives(
     stream,
     queries,
     new_keys,
@@ -92,6 +96,451 @@
     return (stream_out, grad_in, grad_weight)
 
 
+def step_kernel(
+    zs,
+    parts,
+    stream,
+    queries,
+    new_keys,
+    new_values,
+    cache_keys,
+    cache_values,
+    frames,
+    group_index,
+    timestep,
+    gate_table,
+    out_weight_hbm,
+    critic_in_hbm,
+    critic_cot_hbm,
+    weight_shard,
+    stream_out,
+    grad_in_hbm,
+    grad_weight,
+    cin,
+    cot,
+    out_weight,
+    wfull,
+    gmine,
+    psend,
+    precv,
+    dsend,
+    xsend,
+    ysend,
+    rx_diag,
+    ry_diag,
+    rx_block,
+    ry_block,
+    osum,
+    zsend,
+    zrecv,
+    gin,
+    q_all,
+    kfull,
+    vfull,
+    frames_recv,
+    live_row,
+    asend,
+    arecv,
+    ssend,
+    srecv,
+    mixed,
+    send_sems,
+    recv_sems,
+    local_sems,
+):
+    f32, bf16 = jnp.float32, jnp.bfloat16
+    dp, seq = lax.axis_index("dp"), lax.axis_index("seq")
+    z, core = seq // 2, lax.rem(seq, 2)
+    other = 1 - core
+    tokens, width = cin.shape
+    block = width // 4
+    shard = block // (2 * zs)
+    half = width // 2
+    own_q = queries.shape[0]
+    cached, fresh = cache_keys.shape[0], new_keys.shape[0]
+    keys_one = cached + fresh
+    heads_here = half // HEAD
+    zh = zs // 2
+    dp_x = dp + 1 - 2 * lax.rem(dp, 2)
+    dp_y = lax.rem(dp + 2, 4)
+    dp_d = dp_x + 2 - 4 * (dp_x // 2)
+    order = (dp_d, dp_x, dp_y, dp)
+    xn, yn, pair = (dp_x, seq), (dp_y, seq), (dp, z * 2 + other)
+
+    loads = [
+        pltpu.make_async_copy(critic_in_hbm, cin, local_sems.at[0]),
+        pltpu.make_async_copy(critic_cot_hbm, cot, local_sems.at[1]),
+        pltpu.make_async_copy(out_weight_hbm, out_weight, local_sems.at[2]),
+    ]
+    for load in loads:
+        load.start()
+
+    group = []
+    for j in range(zs):
+        for cc in range(2):
+            if j or cc:
+                zt = lax.rem(z + j, zs)
+                ct = core if cc == 0 else other
+                group.append((j, cc, zt, ct))
+    barrier = pltpu.get_barrier_semaphore()
+    peers = [xn, yn] + [(dp, zt * 2 + ct) for (_, _, zt, ct) in group]
+    for peer in peers:
+        pl.semaphore_signal(
+            barrier, inc=1, device_id=peer, device_id_type=pl.DeviceIdType.MESH
+        )
+    pl.semaphore_wait(barrier, len(peers))
+
+    sent = []
+
+    def send(src, dst, peer):
+        n = len(sent)
+        copy = pltpu.make_async_remote_copy(
+            src_ref=src,
+            dst_ref=dst,
+            send_sem=send_sems.at[n],
+            recv_sem=recv_sems.at[n],
+            device_id=peer,
+            device_id_type=pl.DeviceIdType.MESH,
+        )
+        copy.start()
+        sent.append(copy)
+        return copy
+
+    other_cols = pl.ds(pl.multiple_of(other * half, 128), half)
+    own_cols = pl.ds(pl.multiple_of(core * half, 128), half)
+
+    early = []
+    for j, cc, zt, ct in group:
+        cols = own_cols if cc == 0 else other_cols
+        early.append(send(queries.at[:, cols], q_all.at[seq], (dp, zt * 2 + ct)))
+    early.append(
+        send(cache_keys.at[:, other_cols], kfull.at[pl.ds(keys_one, cached)], pair)
+    )
+    early.append(
+        send(new_keys.at[:, other_cols], kfull.at[pl.ds(keys_one + cached, fresh)], pair)
+    )
+    early.append(
+        send(cache_values.at[:, other_cols], vfull.at[pl.ds(keys_one, cached)], pair)
+    )
+    early.append(
+        send(new_values.at[:, other_cols], vfull.at[pl.ds(keys_one + cached, fresh)], pair)
+    )
+    early.append(send(frames, frames_recv, pair))
+    w_z = []
+    for j in range(1, zs):
+        zt = lax.rem(z + j, zs)
+        w_z.append(send(weight_shard, wfull.at[dp, z, core], (dp, zt * 2 + core)))
+
+    wfull[dp, z, core] = weight_shard[...]
+    q_all[seq] = queries[:, own_cols]
+    kfull[0:cached] = cache_keys[:, own_cols]
+    kfull[cached:keys_one] = new_keys[:, own_cols]
+    vfull[0:cached] = cache_values[:, own_cols]
+    vfull[cached:keys_one] = new_values[:, own_cols]
+
+    loads[0].wait()
+    loads[1].wait()
+    tile = 512 if width % 512 == 0 else 128
+
+    def grad_block(b):
+        rows = pl.ds(pl.multiple_of(order[b] * block, 128), block)
+
+        def body(t, carry):
+            cols = pl.ds(pl.multiple_of(t * tile, tile), tile)
+            acc = lax.dot_general(
+                cin[:, rows],
+                cot[:, cols],
+                (((0,), (0,)), ((), ())),
+                preferred_element_type=f32,
+            )
+            for k in range(zs):
+                lo = acc[2 * k * shard : (2 * k + 1) * shard]
+                hi = acc[(2 * k + 1) * shard : (2 * k + 2) * shard]
+                gmine[b, k, :, cols] = jnp.where(core == 0, lo, hi)
+                psend[b, k, :, cols] = jnp.where(core == 0, hi, lo).astype(bf16)
+            return carry
+
+        lax.fori_loop(0, width // tile, body, 0)
+        return send(psend.at[b], precv.at[b], pair)
+
+    def chip_sum(b, k):
+        return gmine[b, k] + precv[b, k].astype(f32)
+
+    pair_d = grad_block(0)
+    pair_x = grad_block(1)
+    pair_d.wait_recv()
+    for k in range(zs):
+        dsend[k] = chip_sum(0, k).astype(bf16)
+    diag_x = send(dsend.at[pl.ds(0, zh)], rx_diag, xn)
+    diag_y = send(dsend.at[pl.ds(zh, zs - zh)], ry_diag, yn)
+    pair_y = grad_block(2)
+    pair_x.wait_recv()
+    for k in range(zh):
+        xsend[k] = chip_sum(1, k).astype(bf16)
+    x_first = send(xsend.at[pl.ds(0, zh)], rx_block.at[pl.ds(0, zh)], xn)
+    pair_y.wait_recv()
+    for k in range(zh, zs):
+        ysend[k] = chip_sum(2, k).astype(bf16)
+    y_second = send(ysend.at[pl.ds(zh, zs - zh)], ry_block.at[pl.ds(zh, zs - zh)], yn)
+    pair_o = grad_block(3)
+    diag_x.wait_recv()
+    for k in range(zh):
+        ysend[k] = (chip_sum(2, k) + rx_diag[k].astype(f32)).astype(bf16)
+    y_first = send(ysend.at[pl.ds(0, zh)], ry_block.at[pl.ds(0, zh)], yn)
+    diag_y.wait_recv()
+    for k in range(zh, zs):
+        xsend[k] = (chip_sum(1, k) + ry_diag[k - zh].astype(f32)).astype(bf16)
+    x_second = send(xsend.at[pl.ds(zh, zs - zh)], rx_block.at[pl.ds(zh, zs - zh)], xn)
+
+    for copy in early:
+        copy.wait_recv()
+    first_frame = FRAMES_GROUP * group_index[0]
+    live_row[...] = jnp.ones_like(live_row)
+    for at, held in ((0, frames), (keys_one, frames_recv)):
+        f = held[...]
+        ok = (f < first_frame) & (f >= first_frame - WINDOW_FRAMES)
+        live_row[:, at : at + cached] = jnp.where(ok, 1.0, 0.0)
+    live = live_row[...] > 0.5
+    rows_q = 2 * zs * own_q
+    lane = lax.broadcasted_iota(jnp.int32, (rows_q, 128), 1)
+    stats = jnp.zeros((rows_q, 128), f32)
+    for h in range(heads_here):
+        cols = slice(h * HEAD, (h + 1) * HEAD)
+        q_head = q_all[:, :, cols].reshape(rows_q, HEAD)
+        scores = lax.dot_general(
+            q_head, kfull[:, cols], (((1,), (1,)), ((), ())), preferred_element_type=f32
+        ) * (HEAD ** (-0.5))
+        scores = jnp.where(live, scores, -1e30)
+        top = jnp.max(scores, axis=1, keepdims=True)
+        weights = jnp.where(live, jnp.exp(scores - top), 0.0)
+        total = jnp.sum(weights, axis=1, keepdims=True)
+        summed = jnp.dot(weights.astype(bf16), vfull[:, cols], preferred_element_type=f32)
+        asend[:, :, cols] = summed.astype(bf16).reshape(2 * zs, own_q, HEAD)
+        stats = jnp.where(lane == h, top, stats)
+        stats = jnp.where(lane == 64 + h, total, stats)
+    ssend[...] = stats.reshape(2 * zs, own_q, 128)
+    late = []
+    for j, cc, zt, ct in group:
+        peer = (dp, zt * 2 + ct)
+        late.append(send(asend.at[zt * 2 + ct], arecv.at[j * 2 + cc], peer))
+        late.append(send(ssend.at[zt * 2 + ct], srecv.at[j * 2 + cc], peer))
+    arecv[0] = asend[seq]
+    srecv[0] = ssend[seq]
+
+    for copy in w_z:
+        copy.wait_recv()
+    mine = wfull.at[dp, :, core]
+    w_x = send(mine, mine, xn)
+    w_y = send(mine, mine, yn)
+    w_p = send(mine, mine, pair)
+
+    stores = []
+
+    def grad_in_block(b):
+        rows = wfull[order[b]].reshape(block, width)
+        step = 256
+
+        def body(t, carry):
+            at = pl.ds(pl.multiple_of(t * step, step), step)
+            gin[b, at] = lax.dot_general(
+                cot[at], rows, (((1,), (1,)), ((), ())), preferred_element_type=f32
+            ).astype(bf16)
+            return carry
+
+        lax.fori_loop(0, tokens // step, body, 0)
+        store = pltpu.make_async_copy(
+            gin.at[b],
+            grad_in_hbm.at[:, pl.ds(pl.multiple_of(order[b] * block, 128), block)],
+            local_sems.at[3 + b],
+        )
+        store.start()
+        stores.append(store)
+
+    w_p.wait_recv()
+    grad_in_block(3)
+
+    pair_o.wait_recv()
+    x_first.wait_recv()
+    x_second.wait_recv()
+    y_first.wait_recv()
+    y_second.wait_recv()
+    for k in range(zs):
+        osum[k] = chip_sum(3, k) + rx_block[k].astype(f32) + ry_block[k].astype(f32)
+    z_parts = []
+    for j in range(1, zs):
+        zt = lax.rem(z + j, zs)
+        zsend[j - 1] = osum[zt].astype(bf16)
+        z_parts.append(send(zsend.at[j - 1], zrecv.at[j - 1], (dp, zt * 2 + core)))
+
+    w_x.wait_recv()
+    from_x = wfull.at[dp_x, :, core]
+    fx = wfull.at[dp_x, pl.ds(0, zh), core]
+    w_fy = send(fx, fx, yn)
+    w_px = send(from_x, from_x, pair)
+    w_y.wait_recv()
+    from_y = wfull.at[dp_y, :, core]
+    fy = wfull.at[dp_y, pl.ds(zh, zs - zh), core]
+    w_fx = send(fy, fy, xn)
+    w_py = send(from_y, from_y, pair)
+
+    for copy in late:
+        copy.wait_recv()
+    for cc in range(2):
+        ct = core if cc == 0 else other
+        for h in range(heads_here):
+            cols = slice(h * HEAD, (h + 1) * HEAD)
+            tops = [srecv[j * 2 + cc][:, h : h + 1] for j in range(zs)]
+            sums = [srecv[j * 2 + cc][:, 64 + h : 65 + h] for j in range(zs)]
+            top = functools.reduce(jnp.maximum, tops)
+            acc = jnp.zeros((own_q, HEAD), f32)
+            total = jnp.zeros((own_q, 1), f32)
+            for j in range(zs):
+                scale = jnp.exp(tops[j] - top)
+                acc = acc + scale * arecv[j * 2 + cc][:, cols].astype(f32)
+                total = total + scale * sums[j]
+            at = pl.ds(pl.multiple_of(ct * half + h * HEAD, 128), HEAD)
+            mixed[:, at] = (acc / total).astype(bf16)
+    loads[2].wait()
+    gate = jnp.zeros((1, width), f32)
+    for s in range(gate_table.shape[0]):
+        gate = gate + jnp.where(timestep[0] == s, gate_table[s : s + 1], 0.0)
+    projected = jnp.dot(mixed[...], out_weight[...], preferred_element_type=f32)
+    stream_out[...] = (stream[...].astype(f32) + gate * projected).astype(bf16)
+
+    w_px.wait_recv()
+    grad_in_block(1)
+    w_py.wait_recv()
+    grad_in_block(2)
+
+    factor = float(tokens * parts) ** (-0.5)
+    for copy in z_parts:
+        copy.wait_recv()
+    grad = osum[z]
+    for j in range(1, zs):
+        grad = grad + zrecv[j - 1].astype(f32)
+    grad_weight[...] = grad * factor
+
+    w_fy.wait_recv()
+    w_fx.wait_recv()
+    from_d = wfull.at[dp_d, :, core]
+    w_pd = send(from_d, from_d, pair)
+    w_pd.wait_recv()
+    grad_in_block(0)
+
+    for copy in sent:
+        copy.wait_send()
+    for store in stores:
+        store.wait()
+
+
+def fused(
+    stream,
+    queries,
+    new_keys,
+    new_values,
+    cache_keys,
+    cache_values,
+    cache_frames,
+    group_index,
+    timestep,
+    gate_table,
+    attn_out_weight,
+    critic_in,
+    critic_cot,
+    critic_weight,
+):
+    bf16, f32 = jnp.bfloat16, jnp.float32
+    zs = lax.axis_size("seq") // 2
+    parts = lax.axis_size(("dp", "seq"))
+    tokens, width = critic_in.shape
+    own_q = queries.shape[1]
+    shard = critic_weight.shape[0]
+    cached, fresh = cache_keys.shape[1], new_keys.shape[1]
+    half = width // 2
+    keys_two = 2 * (cached + fresh)
+    zh = zs // 2
+    messages = 2 * zs + 4 + (zs - 1) + 4 + 2 + 4 + 2 * (2 * zs - 1) + 3 + (zs - 1) + 4 + 1
+    vm = pl.BlockSpec(memory_space=pltpu.VMEM)
+    sm = pl.BlockSpec(memory_space=pltpu.SMEM)
+    hbm = pl.BlockSpec(memory_space=pl.ANY)
+    stream_out, grad_in, grad_weight = pl.pallas_call(
+        functools.partial(step_kernel, zs, parts),
+        out_shape=(
+            jax.ShapeDtypeStruct(stream.shape[1:], bf16),
+            jax.ShapeDtypeStruct((tokens, width), bf16),
+            jax.ShapeDtypeStruct((shard, width), f32),
+        ),
+        in_specs=[vm] * 7 + [sm] * 2 + [vm] + [hbm] * 3 + [vm],
+        out_specs=(vm, hbm, vm),
+        scratch_shapes=[
+            pltpu.VMEM((tokens, width), bf16),
+            pltpu.VMEM((tokens, width), bf16),
+            pltpu.VMEM((width, width), bf16),
+            pltpu.VMEM((4, zs, 2, shard, width), bf16),
+            pltpu.VMEM((4, zs, shard, width), f32),
+            pltpu.VMEM((4, zs, shard, width), bf16),
+            pltpu.VMEM((4, zs, shard, width), bf16),
+            pltpu.VMEM((zs, shard, width), bf16),
+            pltpu.VMEM((zs, shard, width), bf16),
+            pltpu.VMEM((zs, shard, width), bf16),
+            pltpu.VMEM((zh, shard, width), bf16),
+            pltpu.VMEM((zs - zh, shard, width), bf16),
+            pltpu.VMEM((zs, shard, width), bf16),
+            pltpu.VMEM((zs, shard, width), bf16),
+            pltpu.VMEM((zs, shard, width), f32),
+            pltpu.VMEM((zs - 1, shard, width), bf16),
+            pltpu.VMEM((zs - 1, shard, width), bf16),
+            pltpu.VMEM((4, tokens, width // 4), bf16),
+            pltpu.VMEM((2 * zs, own_q, half), bf16),
+            pltpu.VMEM((keys_two, half), bf16),
+            pltpu.VMEM((keys_two, half), bf16),
+            pltpu.VMEM((1, cached), jnp.int32),
+            pltpu.VMEM((1, keys_two), f32),
+            pltpu.VMEM((2 * zs, own_q, half), bf16),
+            pltpu.VMEM((2 * zs, own_q, half), bf16),
+            pltpu.VMEM((2 * zs, own_q, 128), f32),
+            pltpu.VMEM((2 * zs, own_q, 128), f32),
+            pltpu.VMEM((own_q, width), bf16),
+            pltpu.SemaphoreType.DMA((messages,)),
+            pltpu.SemaphoreType.DMA((messages,)),
+            pltpu.SemaphoreType.DMA((7,)),
+        ],
+        compiler_params=pltpu.CompilerParams(
+            collective_id=0, has_side_effects=True, vmem_limit_bytes=60 * 1024 * 1024
+        ),
+    )(
+        stream[0],
+        queries[0],
+        new_keys[0],
+        new_values[0],
+        cache_keys[0],
+        cache_values[0],
+        cache_frames,
+        group_index,
+        timestep,
+        gate_table,
+        attn_out_weight,
+        critic_in,
+        critic_cot,
+        critic_weight,
+    )
+    return (stream_out[None], grad_in, grad_weight)
+
+
+def local(*args):
+    shard, tokens = args[13].shape[0], args[11].shape[0]
+    fits = (
+        lax.axis_size("dp") == 4
+        and lax.axis_size("seq") % 4 == 0
+        and shard % 16 == 0
+        and args[1].shape[1] % 16 == 0
+        and args[4].shape[1] % 16 == 0
+        and args[1].shape[2] % 512 == 0
+        and tokens % 256 == 0
+    )
+    return fused(*args) if fits else by_collectives(*args)
+
+
 def solution(mesh):
     return jax.shard_map(
         local,

time: 288 us -> 70.6 us (0.25); the launches traced: 283 us -> 70.4 us
  waiting for transfers between devices: 181 us -> 0 us
  Pallas kernels: 0 us -> 62.4 us
  blocking collectives: 39 us -> 0 us
  matrix products: 28.5 us -> 0 us
  between operations: 16.8 us -> 1.94 us
  local copies, waits for them, and re-layouts: 15 us -> 6.06 us
  other arithmetic: 2.93 us -> 0 us
    reduce_scatter x1 -> x0, waiting for transfers between devices: 124 us -> none  [critic_pass(): lax.psum_scatter(whole_term, ('dp', 'seq'), scatter_dimension=0, tiled=True)]
    pallas_call x0 -> x1, Pallas kernels: none -> 62.4 us  [fused(): pl.pallas_call(functools.partial(step_kernel, zs, parts), out_shape=(jax....]
    unnamed x6 -> x0, waiting for transfers between devices: 50.8 us -> none
    dot_general x6 -> x0, matrix products: 28.5 us -> none  [the longest x1 9.59 us: critic_pass(): lax.dot_general(critic_in, critic_cot, (((0,), (0,)), ((), ())), preferre...]
    pmax x1 -> x0, blocking collectives: 21.6 us -> none  [local(): global_top = lax.pmax(local_top, 'seq')]
    all_gather x1 -> x0, blocking collectives: 17.4 us -> none  [local(): all_queries = lax.all_gather(queries, 'seq', axis=1, tiled=True)[0]]
    all_gather x1 -> x0, waiting for transfers between devices: 6.06 us -> none  [critic_pass(): lax.all_gather(critic_weight, ('dp', 'seq'), axis=0, tiled=True)]
    unnamed x16 -> x5, local copies, waits for them, and re-layouts: 9.71 us -> 6.06 us
  transfers between devices with their start and end apart: 4 -> 0, of which waited for: 4 -> 0; matrix products, arithmetic and copies ran while one was open for 13% -> 0% of each run, Pallas kernels for 0% -> 0%
where the time goes in v1:
time: 70.6 us; the launch traced here: 70.4 us
  Pallas kernels  62.4 us (88%)
  local copies, waits for them, and re-layouts  6.06 us (9%)
  between operations  1.94 us (3%)
    pallas_call x1, Pallas kernels, fused(): pl.pallas_call(functools.partial(step_kernel, zs, parts), out_shape=(jax....  62.4 us
    unnamed x5, local copies, waits for them, and re-layouts  6.06 us

profile of v1, /device:TPU:9, one launch (start us, length us, event | category | flops | bytes accessed | tf_op | source)
XLA Modules:
  0.0 70.4 jit_solution(17132527542529284225)
XLA Ops:
  1.9 62.4 %shard_map.157 = (bf16[32,1536]{1,0:T(8,128)(2,1)}, bf16[1024,1536]{1,0:T(8,128)(2,1)}, f32[48,1536]{1,0:T(8,128)}) custom-call(bf16[32,1536]{1,0:T(8,128)(2,1)} %bitcast.9, bf16[32,1536]{1,0:T(8,128)(2,1)} %bitcast.10, bf16[32,1536]{1,0:T(8,128)(2,1)} %bitcast.11, bf16[32,1536]{1,0:T(8,128)(2,1)} %bitcast.12, bf16[96,1536]{1,0:T(8,128)(2,1)} %bitcast.7, ...), custom_call_target="tpu_custom_call" | custom-call | tf_op jit(solution)/shard_map/pallas_call | solution.py:466
  64.3 1.5 %copy.22 = bf16[1,32,1536]{2,1,0:T(8,128)(2,1)} copy(bf16[1,32,1536]{2,1,0:T(8,128)(2,1)} %bitcast.13) | data formatting | bytes 196608
  65.9 0.0 copy-start
  65.9 3.8 %copy.23 = bf16[1024,1536]{1,0:T(8,128)(2,1)} copy(bf16[1024,1536]{1,0:T(8,128)(2,1)} %get-tuple-element.13) | data formatting | bytes 6291456
  69.7 0.0 copy-done
  69.7 0.7 %copy.24 = f32[48,1536]{1,0:T(8,128)} copy(f32[48,1536]{1,0:T(8,128)S(1)} %copy-done) | data formatting | bytes 589824
Async XLA Ops:
  65.9 3.8 %copy-start = (f32[48,1536]{1,0:T(8,128)S(1)}, f32[48,1536]{1,0:T(8,128)}, u32[]{:S(2)}) copy-start(f32[48,1536]{1,0:T(8,128)} %get-tuple-element.14) | copy-start | bytes 884740

commit v2 on v1

--- a/solution.py
+++ b/solution.py
@@ -116,6 +116,7 @@
     stream_out,
     grad_in_hbm,
     grad_weight,
+    diag_rows,
     cin,
     cot,
     out_weight,
@@ -213,23 +214,25 @@
     for j, cc, zt, ct in group:
         cols = own_cols if cc == 0 else other_cols
         early.append(send(queries.at[:, cols], q_all.at[seq], (dp, zt * 2 + ct)))
-    early.append(
-        send(cache_keys.at[:, other_cols], kfull.at[pl.ds(keys_one, cached)], pair)
-    )
-    early.append(
-        send(new_keys.at[:, other_cols], kfull.at[pl.ds(keys_one + cached, fresh)], pair)
-    )
-    early.append(
-        send(cache_values.at[:, other_cols], vfull.at[pl.ds(keys_one, cached)], pair)
-    )
-    early.append(
-        send(new_values.at[:, other_cols], vfull.at[pl.ds(keys_one + cached, fresh)], pair)
-    )
-    early.append(send(frames, frames_recv, pair))
-    w_z = []
+    w_z, w_x, w_y, w_p = [], [], [], []
     for j in range(1, zs):
         zt = lax.rem(z + j, zs)
         w_z.append(send(weight_shard, wfull.at[dp, z, core], (dp, zt * 2 + core)))
+    for into, peer in ((w_x, xn), (w_y, yn), (w_p, pair)):
+        into.append(send(weight_shard, wfull.at[dp, z, core], peer))
+    early.append(
+        send(cache_keys.at[:, other_cols], kfull.at[pl.ds(keys_one, cached)], pair)
+    )
+    early.append(
+        send(new_keys.at[:, other_cols], kfull.at[pl.ds(keys_one + cached, fresh)], pair)
+    )
+    early.append(
+        send(cache_values.at[:, other_cols], vfull.at[pl.ds(keys_one, cached)], pair)
+    )
+    early.append(
+        send(new_values.at[:, other_cols], vfull.at[pl.ds(keys_one + cached, fresh)], pair)
+    )
+    early.append(send(frames, frames_recv, pair))
 
     wfull[dp, z, core] = weight_shard[...]
     q_all[seq] = queries[:, own_cols]
@@ -291,6 +294,12 @@
     for k in range(zh, zs):
         xsend[k] = (chip_sum(1, k) + ry_diag[k - zh].astype(f32)).astype(bf16)
     x_second = send(xsend.at[pl.ds(zh, zs - zh)], rx_block.at[pl.ds(zh, zs - zh)], xn)
+
+    for j in range(1, zs):
+        w_z[j - 1].wait_recv()
+        held = wfull.at[dp, lax.rem(z + zs - j, zs), core]
+        for into, peer in ((w_x, xn), (w_y, yn), (w_p, pair)):
+            into.append(send(held, held, peer))
 
     for copy in early:
         copy.wait_recv()
@@ -327,12 +336,20 @@
     arecv[0] = asend[seq]
     srecv[0] = ssend[seq]
 
-    for copy in w_z:
-        copy.wait_recv()
-    mine = wfull.at[dp, :, core]
-    w_x = send(mine, mine, xn)
-    w_y = send(mine, mine, yn)
-    w_p = send(mine, mine, pair)
+    w_px, w_py, w_diag = [], [], []
+
+    def pass_on(j):
+        zf = lax.rem(z + zs - j, zs)
+        w_x[j].wait_recv()
+        held = wfull.at[dp_x, zf, core]
+        if j < zh:
+            w_diag.append(send(held, held, yn))
+        w_px.append(send(held, held, pair))
+        w_y[j].wait_recv()
+        held = wfull.at[dp_y, zf, core]
+        if j >= zh:
+            w_diag.append(send(held, held, xn))
+        w_py.append(send(held, held, pair))
 
     stores = []
 
@@ -356,7 +373,9 @@
         store.start()
         stores.append(store)
 
-    w_p.wait_recv()
+    pass_on(0)
+    for copy in w_p:
+        copy.wait_recv()
     grad_in_block(3)
 
     pair_o.wait_recv()
@@ -372,16 +391,8 @@
         zsend[j - 1] = osum[zt].astype(bf16)
         z_parts.append(send(zsend.at[j - 1], zrecv.at[j - 1], (dp, zt * 2 + core)))
 
-    w_x.wait_recv()
-    from_x = wfull.at[dp_x, :, core]
-    fx = wfull.at[dp_x, pl.ds(0, zh), core]
-    w_fy = send(fx, fx, yn)
-    w_px = send(from_x, from_x, pair)
-    w_y.wait_recv()
-    from_y = wfull.at[dp_y, :, core]
-    fy = wfull.at[dp_y, pl.ds(zh, zs - zh), core]
-    w_fx = send(fy, fy, xn)
-    w_py = send(from_y, from_y, pair)
+    for j in range(1, zs):
+        pass_on(j)
 
     for copy in late:
         copy.wait_recv()
@@ -407,10 +418,17 @@
     projected = jnp.dot(mixed[...], out_weight[...], preferred_element_type=f32)
     stream_out[...] = (stream[...].astype(f32) + gate * projected).astype(bf16)
 
-    w_px.wait_recv()
+    for copy in w_px:
+        copy.wait_recv()
     grad_in_block(1)
-    w_py.wait_recv()
+    for copy in w_py:
+        copy.wait_recv()
     grad_in_block(2)
+    w_pd = []
+    for j in range(zs):
+        w_diag[j].wait_recv()
+        held = wfull.at[dp_d, lax.rem(z + zs - j, zs), core]
+        w_pd.append(send(held, held, pair))
 
     factor = float(tokens * parts) ** (-0.5)
     for copy in z_parts:
@@ -420,17 +438,31 @@
         grad = grad + zrecv[j - 1].astype(f32)
     grad_weight[...] = grad * factor
 
-    w_fy.wait_recv()
-    w_fx.wait_recv()
-    from_d = wfull.at[dp_d, :, core]
-    w_pd = send(from_d, from_d, pair)
-    w_pd.wait_recv()
-    grad_in_block(0)
+    for copy in w_pd:
+        copy.wait_recv()
+    keep = pltpu.make_async_copy(wfull.at[dp_d], diag_rows, local_sems.at[3])
+    keep.start()
+    stores.append(keep)
 
     for copy in sent:
         copy.wait_send()
     for store in stores:
         store.wait()
+
+
+def finish_kernel(stream_part, weight_part, grad_part, cot, diag_rows, stream_out, grad_weight, grad_in):
+    stream_out[...] = stream_part[...]
+    grad_weight[...] = weight_part[...]
+    grad_in[...] = grad_part[...]
+    width = cot.shape[1]
+    block = width // 4
+    dp = lax.axis_index("dp")
+    dp_x = dp + 1 - 2 * lax.rem(dp, 2)
+    dp_d = dp_x + 2 - 4 * (dp_x // 2)
+    rows = diag_rows[...].reshape(block, width)
+    grad_in[:, pl.ds(pl.multiple_of(dp_d * block, 128), block)] = lax.dot_general(
+        cot[...], rows, (((1,), (1,)), ((), ())), preferred_element_type=jnp.float32
+    ).astype(grad_in.dtype)
 
 
 def fused(
@@ -459,19 +491,20 @@
     half = width // 2
     keys_two = 2 * (cached + fresh)
     zh = zs // 2
-    messages = 2 * zs + 4 + (zs - 1) + 4 + 2 + 4 + 2 * (2 * zs - 1) + 3 + (zs - 1) + 4 + 1
+    messages = (2 * zs - 1) * 3 + 5 + (zs - 1) * 2 + 10 + 7 * zs
     vm = pl.BlockSpec(memory_space=pltpu.VMEM)
     sm = pl.BlockSpec(memory_space=pltpu.SMEM)
     hbm = pl.BlockSpec(memory_space=pl.ANY)
-    stream_out, grad_in, grad_weight = pl.pallas_call(
+    stream_part, grad_part, weight_part, diag_rows = pl.pallas_call(
         functools.partial(step_kernel, zs, parts),
         out_shape=(
             jax.ShapeDtypeStruct(stream.shape[1:], bf16),
             jax.ShapeDtypeStruct((tokens, width), bf16),
             jax.ShapeDtypeStruct((shard, width), f32),
+            jax.ShapeDtypeStruct((zs, 2, shard, width), bf16),
         ),
         in_specs=[vm] * 7 + [sm] * 2 + [vm] + [hbm] * 3 + [vm],
-        out_specs=(vm, hbm, vm),
+        out_specs=(vm, hbm, vm, hbm),
         scratch_shapes=[
             pltpu.VMEM((tokens, width), bf16),
             pltpu.VMEM((tokens, width), bf16),
@@ -524,6 +557,24 @@
         critic_cot,
         critic_weight,
     )
+    rows = 256
+
+    def whole(shape):
+        return pl.BlockSpec(shape, lambda i: (0,) * len(shape))
+
+    tiles = pl.BlockSpec((rows, width), lambda i: (i, 0))
+    small = [whole((own_q, width)), whole((shard, width))]
+    stream_out, grad_weight, grad_in = pl.pallas_call(
+        finish_kernel,
+        grid=(tokens // rows,),
+        out_shape=(
+            jax.ShapeDtypeStruct((own_q, width), bf16),
+            jax.ShapeDtypeStruct((shard, width), f32),
+            jax.ShapeDtypeStruct((tokens, width), bf16),
+        ),
+        in_specs=small + [tiles, tiles, whole((zs, 2, shard, width))],
+        out_specs=tuple(small + [tiles]),
+    )(stream_part, weight_part, grad_part, critic_cot, diag_rows)
     return (stream_out[None], grad_in, grad_weight)
 
 

time: 70.6 us -> 66.7 us (0.945)
  the two profiles are of different devices: /device:TPU:9 before, /device:TPU:31 now
where the time goes in v2:
time: 66.7 us; the launch traced here: 66.5 us
  Pallas kernels  64.6 us (97%)
  between operations  1.93 us (3%)
    pallas_call x1, Pallas kernels, fused(): pl.pallas_call(functools.partial(step_kernel, zs, parts), out_shape=(jax....  58.1 us
    pallas_call x1, Pallas kernels, fused(): pl.pallas_call(finish_kernel, grid=(tokens // rows,), out_shape=(jax.Shap...  6.55 us

profile of v2, /device:TPU:31, one launch (start us, length us, event | category | flops | bytes accessed | tf_op | source)
XLA Modules:
  0.0 66.5 jit_solution(4859075833143629643)
XLA Ops:
  1.9 58.1 %shard_map.157 = (bf16[32,1536]{1,0:T(8,128)(2,1)}, bf16[1024,1536]{1,0:T(8,128)(2,1)}, f32[48,1536]{1,0:T(8,128)}, bf16[4,2,48,1536]{3,2,1,0:T(8,128)(2,1)}) custom-call(bf16[32,1536]{1,0:T(8,128)(2,1)} %bitcast.9, bf16[32,1536]{1,0:T(8,128)(2,1)} %bitcast.10, bf16[32,1536]{1,0:T(8,128)(2,1)} %bitcast.11, bf16[32,1536]{1,0:T(8,128)(2,1)} %bitcast.12, ...), custom_call_target="tpu_custom_call" | custom-call | tf_op jit(solution)/shard_map/pallas_call | solution.py:498
  60.0 6.6 %shard_map.158 = (bf16[32,1536]{1,0:T(8,128)(2,1)}, f32[48,1536]{1,0:T(8,128)}, bf16[1024,1536]{1,0:T(8,128)(2,1)}) custom-call(bf16[32,1536]{1,0:T(8,128)(2,1)} %get-tuple-element.10.stream_part, f32[48,1536]{1,0:T(8,128)} %get-tuple-element.11.weight_part, bf16[1024,1536]{1,0:T(8,128)(2,1)} %get-tuple-element.12.grad_part, bf16[1024,1536]{1,0:T(8,128)(2,1)} %cot.1, ...), custom_call_target="tpu_custom_call" | custom-call | tf_op jit(solution)/shard_map/pallas_call | solution.py:567
